TPU v7x, 32 devices: a whole 2x2x4 slice. The times are simulated.
32 devices in a mesh: group: 16 (over z, y, core), helper: 2 (over x).
Axes of the slice: x: 2, y: 2, z: 4, core: 2. Of those that a mesh axis runs over, the one named last changes fastest.
Arguments:
- candidates: bfloat16 [16, 512, 1024], P('group', 'helper'), may hold values from -6 to 6
- prefix_cache: bfloat16 [16, 2, 768, 1024], P('group', None, 'helper'), may hold values from -6 to 6
- w_uvqk: bfloat16 [1024, 4096], replicated, may hold values from -0.1875 to 0.1875
- w_output: bfloat16 [1024, 1024], replicated, may hold values from -0.1875 to 0.1875
- norm_gain: float32 [1024], replicated, may hold values from 0.1 to 1.9
- owner: int32 [16], replicated, may hold values from 0 to 15, as said below
- counts: int32 [16], replicated, may hold values from 256 to 512, as said below
- prefix_len: int32 [16], replicated, may hold values from 24 to 768, as said below
Outputs:
- update: bfloat16 [16, 512, 1024], P('group', 'helper')
Inputs may be any that keep to these rules, and one draw needn't show every extreme that they name: owner[u] = (u + s) mod 16 for one shift s of the round. `counts`: multiples of 128; some user has exactly 512. `prefix_len`: some user has exactly 768.
All inputs are finite; a program needn't handle non-finite values.
Results may differ from a plain program's by a relative error of at most 0.012.
Values may be sent and summed in bfloat16 or wider, within the bound.
A program may use at most 128 MiB of HBM per device.

v0:
```python
import math

import jax
import jax.numpy as jnp
from jax import lax
from jax.sharding import PartitionSpec as P

HEADS = 8


def from_behind(value, axis, steps):
    count = lax.axis_size(axis)
    pairs = [(source, (source + steps) % count) for source in range(count)]
    return lax.ppermute(value, axis, pairs)


def pick(table, index):
    places = jnp.arange(table.shape[0], dtype=jnp.int32)
    return jnp.sum(jnp.where(places == index, table, 0))


def local(candidates, prefix_cache, w_uvqk, w_output, norm_gain, owner, counts, prefix_len):
    groups = lax.axis_size("group")
    group_here = lax.axis_index("group")
    helper_here = lax.axis_index("helper")
    levels = groups.bit_length() - 1
    offset = owner[0]
    slots = candidates.shape[1]
    width = candidates.shape[2]
    head = width // HEADS
    scale = head ** (-0.5)
    tokens = candidates[0]
    for level in range(levels):
        moved = from_behind(tokens, "group", 1 << level)
        tokens = jnp.where(offset >> level & 1 == 1, moved, tokens)
    user = (group_here - offset) % groups
    count = pick(counts, user)
    visible = pick(prefix_len, user)
    live = jnp.clip(count - helper_here * slots, 0, slots)
    proj = jax.nn.silu(jnp.dot(tokens, w_uvqk, preferred_element_type=jnp.float32))
    gate_u = proj[:, :width]
    own_v = proj[:, width : 2 * width].astype(jnp.bfloat16).reshape(slots, HEADS, head)
    query = proj[:, 2 * width : 3 * width].astype(jnp.bfloat16).reshape(slots, HEADS, head)
    own_k = proj[:, 3 * width :].astype(jnp.bfloat16).reshape(slots, HEADS, head)
    block = math.gcd(slots, 128)
    blocks_live = (live + block - 1) // block
    start_acc = jnp.zeros((slots, width), jnp.float32)
    piece = lax.all_gather(prefix_cache, "helper", axis=2, tiled=True)
    length = piece.shape[2]
    keys4 = piece[0, 0].reshape(length, HEADS, head)
    values4 = piece[0, 1].reshape(length, HEADS, head)
    allowed = jnp.arange(length, dtype=jnp.int32) < visible

    def one_block(number, acc):
        first = number * block
        query_block = lax.dynamic_slice_in_dim(query, first, block, 0)
        scores = (
            jnp.einsum("rhd,nhd->hrn", query_block, keys4, preferred_element_type=jnp.float32)
            * scale
        )
        weights = jnp.where(allowed[None, None, :], jax.nn.silu(scores), 0.0).astype(jnp.bfloat16)
        partial_block = jnp.einsum(
            "hrn,nhd->rhd", weights, values4, preferred_element_type=jnp.float32
        )
        old = lax.dynamic_slice_in_dim(acc, first, block, 0)
        return lax.dynamic_update_slice_in_dim(
            acc, old + partial_block.reshape(block, width), first, 0
        )

    mixed = lax.fori_loop(0, blocks_live, one_block, start_acc)
    selfw = jax.nn.silu(
        jnp.einsum("rhd,rhd->rh", query, own_k, preferred_element_type=jnp.float32) * scale
    ).astype(jnp.bfloat16)
    mixed = mixed + (selfw.astype(jnp.float32)[:, :, None] * own_v.astype(jnp.float32)).reshape(
        slots, width
    )
    centre = mixed - jnp.mean(mixed, axis=-1, keepdims=True)
    spread = jnp.mean(centre * centre, axis=-1, keepdims=True)
    normed = (centre * lax.rsqrt(spread + 1e-05) * norm_gain * gate_u).astype(jnp.bfloat16)
    result = jnp.dot(normed, w_output, preferred_element_type=jnp.float32)
    alive = jnp.arange(slots, dtype=jnp.int32) < live
    result = jnp.where(alive[:, None], result, 0.0).astype(jnp.bfloat16)
    return result[None]


def solution(mesh):
    in_specs = (
        P("group", "helper", None),
        P("group", None, "helper", None),
        P(),
        P(),
        P(),
        P(),
        P(),
        P(),
    )
    out_specs = P("group", "helper", None)
    return jax.shard_map(local, mesh=mesh, in_specs=in_specs, out_specs=out_specs, check_vma=False)
```

profile of v0, /device:TPU:0, one launch (start us, length us, event | category | flops | bytes accessed | tf_op | source)
XLA Modules:
  0.0 117.4 jit_solution(1869276192214609576)
XLA Ops:
  6.5 0.0 copy-start
  6.5 0.5 collective-permute-start
  7.8 11.3 %collective-permute-done = bf16[256,1024]{1,0:T(8,128)(2,1)S(1)} collective-permute-done((bf16[256,1024]{1,0:T(8,128)(2,1)}, bf16[256,1024]{1,0:T(8,128)(2,1)S(1)}, u32[]{:S(2)}, u32[]{:S(2)}) %collective-permute-start) | collective-permute-done | bytes 524320 | tf_op jit(solution)/shard_map/ppermute | solution.py:14
  19.1 1.1 broadcast_select_fusion
  20.2 0.1 collective-permute-start.1
  20.3 2.6 %copy.18 = bf16[1,2,384,1024]{2,3,1,0:T(8,128)(2,1)} copy(bf16[1,2,384,1024]{3,2,1,0:T(8,128)(2,1)} %param.11) | data formatting | bytes 3145728 | tf_op args[1]
  22.9 0.0 all-gather.2.cloned.1.call-update
  22.9 11.0 %collective-permute-done.1 = bf16[256,1024]{1,0:T(8,128)(2,1)} collective-permute-done((bf16[256,1024]{1,0:T(8,128)(2,1)S(1)}, bf16[256,1024]{1,0:T(8,128)(2,1)}, u32[]{:S(2)}, u32[]{:S(2)}) %collective-permute-start.1) | collective-permute-done | bytes 524320 | tf_op jit(solution)/shard_map/ppermute | solution.py:14
  33.9 0.1 broadcast_select_fusion.1
  33.9 0.1 collective-permute-start.2
  34.0 11.8 %collective-permute-done.2 = bf16[256,1024]{1,0:T(8,128)(2,1)} collective-permute-done((bf16[256,1024]{1,0:T(8,128)(2,1)S(1)}, bf16[256,1024]{1,0:T(8,128)(2,1)}, u32[]{:S(2)}, u32[]{:S(2)}) %collective-permute-start.2) | collective-permute-done | bytes 524320 | tf_op jit(solution)/shard_map/ppermute | solution.py:14
  45.9 1.1 broadcast_select_fusion.2
  47.0 0.4 collective-permute-start.3
  47.5 0.6 fusion.23
  48.8 19.5 %collective-permute-done.3 = bf16[256,1024]{1,0:T(8,128)(2,1)S(1)} collective-permute-done((bf16[256,1024]{1,0:T(8,128)(2,1)S(1)}, bf16[256,1024]{1,0:T(8,128)(2,1)S(1)}, u32[]{:S(2)}, u32[]{:S(2)}) %collective-permute-start.3) | collective-permute-done | bytes 524320 | tf_op jit(solution)/shard_map/ppermute | solution.py:14
  68.3 7.8 %fusion.28 = (bf16[256,4096]{1,0:T(8,128)(2,1)S(1)}, f32[256,4096]{1,0:T(8,128)}) fusion(bf16[1024,4096]{1,0:T(8,128)(2,1)} %param.12, bf16[256,1024]{1,0:T(8,128)(2,1)S(1)} %collective-permute-done.3, bf16[256,1024]{1,0:T(8,128)(2,1)S(1)} %broadcast_select_fusion.2, pred[]{:T(512)S(6)} %eq.24), kind=kOutput, calls=%fused_computation.45 | convolution fusion | flops 2152988672 | bytes 15728641 | tf_op jit(solution)/shard_map/dot_general | solution.py:40
  76.1 0.1 slice_bitcast_fusion
  76.2 0.1 copy.37
  76.3 1.2 %copy.36 = bf16[32,8,8,128]{3,2,1,0:T(8,128)(2,1)} copy(bf16[32,8,8,128]{3,1,2,0:T(8,128)(2,1)S(1)} %get-tuple-element.102) | data formatting | bytes 1048576
  77.5 0.1 copy-done.1
  77.7 1.4 %fusion.12 = f32[256,8]{1,0:T(8,128)S(1)} fusion(bf16[256,8,128]{2,1,0:T(8,128)(2,1)} %bitcast.9, bf16[256,8,128]{2,1,0:T(8,128)(2,1)S(1)} %bitcast.36), kind=kLoop, calls=%fused_computation.21 | loop fusion | flops 1046528 | bytes 1056768
  79.1 0.1 copy.28
  79.2 0.1 copy.22
  79.3 0.0 all-gather.2.cloned.1.call-done
  79.3 3.7 %fusion.27 = (bf16[1,1,768,1024]{2,3,1,0:T(8,128)(2,1)}, bf16[1,1,768,1024]{2,3,1,0:T(8,128)(2,1)}) fusion(bf16[1,2,768,1024]{2,3,1,0:T(8,128)(2,1)} %all-gather.2.cloned.1.call-done), kind=kLoop, calls=%fused_computation.44 | loop fusion | bytes 6291456 | tf_op jit(solution)/shard_map/slice | solution.py:51
  83.0 2.6 %copy.21 = bf16[768,8,128]{2,0,1:T(8,128)(2,1)} copy(bf16[768,8,128]{0,2,1:T(8,128)(2,1)} %bitcast.34) | data formatting | bytes 3145728
  85.6 1.1 broadcast_in_dim.41.clone2
  86.8 18.6 %while.11 = (s32[]{:T(128)}, f32[256,1024]{1,0:T(8,128)}, s32[]{:T(128)}, bf16[256,8,128]{2,1,0:T(8,128)(2,1)}, bf16[768,8,128]{2,0,1:T(8,128)(2,1)}, /*index=5*...) while((s32[]{:T(128)}, f32[256,1024]{1,0:T(8,128)}, ...), condition=%wide.region_3.4_spmd.clone, body=%wide.region_2.3_spmd.clone.sunk | while | flops 408290048 | bytes 10225323 | solution.py:70
  86.8 0.6 iota_compare_fusion.3
  87.4 1.0 constant_dynamic-slice_fusion.5
  88.4 4.3 %fusion.40 = f32[8,128,128]{1,2,0:T(8,128)} fusion(bf16[768,8,128]{0,2,1:T(8,128)(2,1)} %get-tuple-element.178, bf16[768,8,128]{2,0,1:T(8,128)(2,1)} %get-tuple-element.177, pred[768]{0:T(1024)(128)(4,1)S(1)} %iota_compare_fusion.3, bf16[128,8,128]{2,1,0:T(8,128)(2,1)S(1)} %constant_dynamic-slice_fusion.5), kind=kOutput, calls=%fused_computation.2.clone.1 | convolution fusion | flops 408158208 | bytes 3932928 | tf_op jit(solution)/shard_map/while/body/hrn,nhd->rhd/dot_general | solution.py:62
  92.6 1.1 constant_dynamic-slice_fusion.4
  93.7 0.2 copy.48
  93.9 1.1 bitcast_add_fusion.2
  95.0 0.2 copy.49
  95.2 0.8 constant_dynamic-update-slice_fusion.2
  96.1 0.6 iota_compare_fusion.3
  96.7 1.0 constant_dynamic-slice_fusion.5
  97.7 4.3 %fusion.40 = f32[8,128,128]{1,2,0:T(8,128)} fusion(bf16[768,8,128]{0,2,1:T(8,128)(2,1)} %get-tuple-element.178, bf16[768,8,128]{2,0,1:T(8,128)(2,1)} %get-tuple-element.177, pred[768]{0:T(1024)(128)(4,1)S(1)} %iota_compare_fusion.3, bf16[128,8,128]{2,1,0:T(8,128)(2,1)S(1)} %constant_dynamic-slice_fusion.5), kind=kOutput, calls=%fused_computation.2.clone.1 | convolution fusion | flops 408158208 | bytes 3932928 | tf_op jit(solution)/shard_map/while/body/hrn,nhd->rhd/dot_general | solution.py:62
  102.0 1.1 constant_dynamic-slice_fusion.4
  103.0 0.2 copy.48
  103.2 1.1 bitcast_add_fusion.2
  104.3 0.2 copy.49
  104.5 0.9 constant_dynamic-update-slice_fusion.2
  105.4 0.3 mul.65
  105.7 1.7 %fusion.25 = (f32[256]{0:T(256)S(1)}, f32[256,1024]{1,0:T(8,128)S(1)}) fusion(f32[256,1024]{1,0:T(8,128)} %get-tuple-element.43, bf16[256,4096]{1,0:T(8,128)(2,1)} %copy-done.1, f32[32,8,8,128]{3,2,1,0:T(8,128)S(1)} %bitcast.35), kind=kLoop, calls=%fused_computation.43 | loop fusion | flops 1048320 | bytes 3671040 | tf_op jit(solution)/shard_map/reduce_sum | solution.py:77
  107.4 0.2 multiply_reduce_fusion
  107.7 2.8 %fusion.9 = bf16[1,256,1024]{2,1,0:T(8,128)(2,1)} fusion(bf16[1024,1024]{1,0:T(8,128)(2,1)S(1)} %copy-done, f32[256,4096]{1,0:T(8,128)} %get-tuple-element.104, f32[256,1024]{1,0:T(8,128)S(1)} %get-tuple-element.98, f32[1024]{0:T(1024)S(1)} %copy-done.2, f32[256]{0:T(256)S(1)} %add_rsqrt_fusion, f32[256]{0:T(256)S(1)} %broadcast_multiply_fusion, ...), kind=kOutput, calls=%fused_computation.15 | convolution fusion | flops 538705920 | bytes 4724992 | tf_op jit(solution)/shard_map/dot_general | solution.py:80
  (15 shorter events, 0.1 us)
Async XLA Ops:
  6.5 101.2 %copy-start = (bf16[1024,1024]{1,0:T(8,128)(2,1)S(1)}, bf16[1024,1024]{1,0:T(8,128)(2,1)}, u32[]{:S(2)}) copy-start(bf16[1024,1024]{1,0:T(8,128)(2,1)} %param.13) | copy-start | bytes 6291460
  6.5 72.8 %all-gather.2.cloned.1.call-start = ((), (), s32[]{:S(2)}) async-start(), calls=%async_computation | async-start | bytes 4718592 | tf_op jit(solution)/shard_map/all_gather | solution.py:48
  6.5 12.5 %collective-permute-start = (bf16[256,1024]{1,0:T(8,128)(2,1)}, bf16[256,1024]{1,0:T(8,128)(2,1)S(1)}, u32[]{:S(2)}, u32[]{:S(2)}) collective-permute-start(bf16[256,1024]{1,0:T(8,128)(2,1)} %bitcast.38), channel_id=1, source_target_pairs={{0,2},{2,4},{4,6},{6,8},{8,10},{10,12},{12,14},{14,16},{16,18},{18... | collective-permute-start | bytes 1572872 | tf_op jit(solution)/shard_map/ppermute | solution.py:14
  7.8 15.1 %copy-start.5 = (s32[16]{0:T(128)S(1)}, s32[16]{0:T(128)}, u32[]{:S(2)}) copy-start(s32[16]{0:T(128)} %param.15) | copy-start | bytes 196
  20.2 13.7 %collective-permute-start.1 = (bf16[256,1024]{1,0:T(8,128)(2,1)S(1)}, bf16[256,1024]{1,0:T(8,128)(2,1)}, u32[]{:S(2)}, u32[]{:S(2)}) collective-permute-start(bf16[256,1024]{1,0:T(8,128)(2,1)S(1)} %broadcast_select_fusion), channel_id=1, source_target_pairs={{0,4},{2,6},{4,8},{6,10},{8,12},{10,14},{12,16},{14,18},{16,20},{1... | collective-permute-start | bytes 1572872 | tf_op jit(solution)/shard_map/ppermute | solution.py:14
  22.9 24.6 %copy-start.3 = (s32[16]{0:T(128)S(1)}, s32[16]{0:T(128)}, u32[]{:S(2)}) copy-start(s32[16]{0:T(128)} %param.16) | copy-start | bytes 196
  22.9 24.6 %copy-start.4 = (s32[16]{0:T(128)S(1)}, s32[16]{0:T(128)}, u32[]{:S(2)}) copy-start(s32[16]{0:T(128)} %param.17) | copy-start | bytes 196
  33.9 11.9 %collective-permute-start.2 = (bf16[256,1024]{1,0:T(8,128)(2,1)S(1)}, bf16[256,1024]{1,0:T(8,128)(2,1)}, u32[]{:S(2)}, u32[]{:S(2)}) collective-permute-start(bf16[256,1024]{1,0:T(8,128)(2,1)S(1)} %broadcast_select_fusion.1), channel_id=1, source_target_pairs={{0,8},{2,10},{4,12},{6,14},{8,16},{10,18},{12,20},{14,22},{16,24},... | collective-permute-start | bytes 1572872 | tf_op jit(solution)/shard_map/ppermute | solution.py:14
  47.0 21.3 %collective-permute-start.3 = (bf16[256,1024]{1,0:T(8,128)(2,1)S(1)}, bf16[256,1024]{1,0:T(8,128)(2,1)S(1)}, u32[]{:S(2)}, u32[]{:S(2)}) collective-permute-start(bf16[256,1024]{1,0:T(8,128)(2,1)S(1)} %broadcast_select_fusion.2), channel_id=1, source_target_pairs={{0,16},{2,18},{4,20},{6,22},{8,24},{10,26},{12,28},{14,30},{16,0},... | collective-permute-start | bytes 1572872 | tf_op jit(solution)/shard_map/ppermute | solution.py:14
  76.1 1.6 %copy-start.1 = (bf16[256,4096]{1,0:T(8,128)(2,1)}, bf16[256,4096]{1,0:T(8,128)(2,1)S(1)}, u32[]{:S(2)}) copy-start(bf16[256,4096]{1,0:T(8,128)(2,1)S(1)} %get-tuple-element.103) | copy-start | bytes 6291460
  105.4 2.3 %copy-start.2 = (f32[1024]{0:T(1024)S(1)}, f32[1024]{0:T(1024)}, u32[]{:S(2)}) copy-start(f32[1024]{0:T(1024)} %param.14) | copy-start | bytes 12292
Sparse Core Ops, SparseCore 0:
  23.0 46.7 all-gather.1
where the time goes:
time: 119 us; the launch traced here: 117 us
  waiting for transfers between devices  53.5 us (45%)
  matrix products  19.2 us (16%)
  local copies, waits for them, and re-layouts  18.7 us (16%)
  between operations  15.2 us (13%)
  other arithmetic  9.73 us (8%)
    ppermute x4, waiting for transfers between devices, from_behind(): return lax.ppermute(value, axis, pairs)  53.5 us
    dot_general x2, matrix products, one_block(): jnp.einsum('hrn,nhd->rhd', weights, values4, preferred_element_type=jnp.f...  8.54 us
    dot_general x1, matrix products, local(): jnp.dot(tokens, w_uvqk, preferred_element_type=jnp.float32)  7.82 us
    unnamed x17, local copies, waits for them, and re-layouts  6.75 us
    slice x1, local copies, waits for them, and re-layouts, local(): values4 = piece[0, 1].reshape(length, HEADS, head)  3.71 us
    dot_general x1, matrix products, local(): result = jnp.dot(normed, w_output, preferred_element_type=jnp.float32)  2.84 us
    dynamic_slice x4, local copies, waits for them, and re-layouts, one_block(): old = lax.dynamic_slice_in_dim(acc, first, block, 0)  2.53 us
  transfers between devices with their start and end apart: 5, of which 4 were waited for; matrix products, arithmetic and copies ran while one was open for 13% of the time, Pallas kernels for 0%

commit v1 on v0

v1 whole, which is shorter than its diff:
```python
import functools
import math

import jax
import jax.numpy as jnp
from jax import lax
from jax.experimental import pallas as pl
from jax.experimental.pallas import tpu as pltpu
from jax.sharding import PartitionSpec as P

HEADS = 8
EPS = 1e-05


def pick(table, index):
    places = jnp.arange(table.shape[0], dtype=jnp.int32)
    return jnp.sum(jnp.where(places == index, table, 0))


def silu(v):
    t = v * 0.5
    return t + t * jnp.tanh(t)


def attend(query, keys, values, scale):
    scores = lax.dot_general(
        query, keys, (((1,), (1,)), ((), ())), preferred_element_type=jnp.float32
    )
    t = scores * (0.5 * scale)
    weights = (t + t * jnp.tanh(t)).astype(jnp.bfloat16)
    return jnp.dot(weights, values, preferred_element_type=jnp.float32)


def seen(values, base, visible):
    rows = lax.broadcasted_iota(jnp.int32, values.shape, 0) + base
    return jnp.where(rows < visible, values, jnp.zeros_like(values))


def first_kernel(head, scale, info, tok, wu, wv, wq, wk, kref, vref, u_out, q_out, acc_out):
    tokens = tok[...]
    u_out[...] = silu(jnp.dot(tokens, wu[...], preferred_element_type=jnp.float32))
    own_v = silu(jnp.dot(tokens, wv[...], preferred_element_type=jnp.float32)).astype(jnp.bfloat16)
    query = silu(jnp.dot(tokens, wq[...], preferred_element_type=jnp.float32)).astype(jnp.bfloat16)
    own_k = silu(jnp.dot(tokens, wk[...], preferred_element_type=jnp.float32)).astype(jnp.bfloat16)
    q_out[...] = query
    prod = query.astype(jnp.float32) * own_k.astype(jnp.float32)
    own_v = own_v.astype(jnp.float32)
    values = seen(vref[...], info[2], info[0])
    for n in range(query.shape[1] // head):
        cols = slice(n * head, (n + 1) * head)
        selfw = silu(jnp.sum(prod[:, cols], axis=1, keepdims=True) * scale)
        selfw = selfw.astype(jnp.bfloat16).astype(jnp.float32)
        mixed = attend(query[:, cols], kref[:, cols], values[:, cols], scale)
        acc_out[:, cols] = mixed + selfw * own_v[:, cols]


def last_kernel(head, scale, pieces, info, q, acc, u, gain, w_out, *rest):
    kvs, out, total = rest[: 2 * pieces], rest[2 * pieces], rest[2 * pieces + 1]
    step = pl.program_id(0)
    wide = q.shape[1]
    mixed = [acc[:, n * head : (n + 1) * head] for n in range(wide // head)]
    for p in range(pieces):
        kref, vref = kvs[2 * p], kvs[2 * p + 1]
        values = seen(vref[...], info[3 + p], info[0])
        for n in range(wide // head):
            cols = slice(n * head, (n + 1) * head)
            mixed[n] += attend(q[:, cols], kref[:, cols], values[:, cols], scale)
    for n in range(wide // head):
        start = pl.multiple_of(step * wide + n * head, head)
        total[:, pl.ds(start, head)] = mixed[n]

    @pl.when(step == pl.num_programs(0) - 1)
    def _():
        a = total[...]
        centre = a - jnp.mean(a, axis=-1, keepdims=True)
        spread = jnp.mean(centre * centre, axis=-1, keepdims=True)
        normed = (centre * lax.rsqrt(spread + EPS) * gain[...] * u[...]).astype(jnp.bfloat16)
        result = jnp.dot(normed, w_out[...], preferred_element_type=jnp.float32)
        rows = lax.broadcasted_iota(jnp.int32, result.shape, 0)
        out[...] = jnp.where(rows < info[1], result, 0.0).astype(jnp.bfloat16)


def local(candidates, prefix_cache, w_uvqk, w_output, norm_gain, owner, counts, prefix_len):
    groups = lax.axis_size("group")
    helpers = lax.axis_size("helper")
    group_here = lax.axis_index("group")
    helper_here = lax.axis_index("helper")
    offset = owner[0]
    _, slots, width = candidates.shape
    length = prefix_cache.shape[2]
    head = width // HEADS
    scale = head ** (-0.5)
    cache = prefix_cache.reshape(2, length, width)
    got = [
        lax.ppermute(cache, "helper", [(i, (i + j) % helpers) for i in range(helpers)])
        for j in range(1, helpers)
    ]

    def turn(s):
        pairs = [(i, (i + s) % groups) for i in range(groups)]
        return lambda t: lax.ppermute(t, "group", pairs) if s else t

    tokens = lax.switch(offset, [turn(s) for s in range(groups)], candidates[0])
    user = (group_here - offset) % groups
    count = pick(counts, user)
    visible = pick(prefix_len, user)
    live = jnp.clip(count - helper_here * slots, 0, slots)
    bases = [((helper_here - j) % helpers) * length for j in range(helpers)]
    info = jnp.stack([visible, live] + bases).astype(jnp.int32)

    wide = 2 * head
    steps = width // wide
    smem = pl.BlockSpec(memory_space=pltpu.SMEM)
    block = lambda rows: pl.BlockSpec((rows, wide), lambda i: (0, i))
    whole = lambda *shape: pl.BlockSpec(shape, lambda i: (0,) * len(shape))
    part = lambda k: pl.BlockSpec((None, length, wide), lambda i: (k, 0, i))
    weight = lambda k: pl.BlockSpec((width, wide), lambda i: (0, k * steps + i))
    gate_u, query, acc = pl.pallas_call(
        functools.partial(first_kernel, head, scale),
        grid=(steps,),
        in_specs=[smem, whole(slots, width)]
        + [weight(k) for k in range(4)]
        + [part(0), part(1)],
        out_specs=[block(slots)] * 3,
        out_shape=[
            jax.ShapeDtypeStruct((slots, width), jnp.float32),
            jax.ShapeDtypeStruct((slots, width), jnp.bfloat16),
            jax.ShapeDtypeStruct((slots, width), jnp.float32),
        ],
        cost_estimate=pl.CostEstimate(
            flops=2 * slots * width * (4 * width + 2 * length),
            bytes_accessed=8 * width * width + 4 * length * width + 12 * slots * width,
            transcendentals=slots * (4 * width + HEADS * length),
        ),
        compiler_params=pltpu.CompilerParams(dimension_semantics=("arbitrary",)),
        name="first",
    )(info, tokens, w_uvqk, w_uvqk, w_uvqk, w_uvqk, cache, cache)
    pieces = helpers - 1
    result = pl.pallas_call(
        functools.partial(last_kernel, head, scale, pieces),
        grid=(steps,),
        in_specs=[
            smem,
            block(slots),
            block(slots),
            whole(slots, width),
            whole(1, width),
            whole(width, width),
        ]
        + [part(0), part(1)] * pieces,
        out_specs=whole(slots, width),
        out_shape=jax.ShapeDtypeStruct((slots, width), jnp.bfloat16),
        scratch_shapes=[pltpu.VMEM((slots, width), jnp.float32)],
        cost_estimate=pl.CostEstimate(
            flops=2 * slots * width * (width + 2 * length * pieces),
            bytes_accessed=2 * width * width + 4 * length * width * pieces + 12 * slots * width,
            transcendentals=slots * HEADS * length * pieces,
        ),
        compiler_params=pltpu.CompilerParams(dimension_semantics=("arbitrary",)),
        name="last",
    )(info, query, acc, gate_u, norm_gain.reshape(1, width), w_output, *[g for g in got for _ in (0, 1)])
    return result[None]


def solution(mesh):
    in_specs = (
        P("group", "helper", None),
        P("group", None, "helper", None),
        P(),
        P(),
        P(),
        P(),
        P(),
        P(),
    )
    out_specs = P("group", "helper", None)
    return jax.shard_map(local, mesh=mesh, in_specs=in_specs, out_specs=out_specs, check_vma=False)
```

time: 119 us -> 47.2 us (0.40); the launches traced: 117 us -> 46.8 us
  waiting for transfers between devices: 53.5 us -> 20.1 us
  matrix products: 19.2 us -> 0 us
  local copies, waits for them, and re-layouts: 18.7 us -> 2.24 us
  Pallas kernels: 0 us -> 15.2 us
  between operations: 15.2 us -> 2.02 us
  other arithmetic: 9.73 us -> 2.55 us
  starting transfers between devices: 1.03 us -> 4.71 us
    ppermute x4 -> x2, waiting for transfers between devices: 53.5 us -> 20.1 us  [the longest x1 19 us: turn(): return lambda t: lax.ppermute(t, 'group', pairs) if s else t]
    dot_general x4 -> x0, matrix products: 19.2 us -> none  [the longest x2 8.54 us: one_block(): jnp.einsum('hrn,nhd->rhd', weights, values4, preferred_element_type=jnp.f...]
    pallas_call x0 -> x2, Pallas kernels: none -> 15.2 us  [the longest x1 8.15 us: local(): pl.pallas_call(functools.partial(first_kernel, head, scale), grid=(steps,...]
    unnamed x17 -> x3, local copies, waits for them, and re-layouts: 6.75 us -> 2.21 us
    dynamic_slice x6 -> x0, local copies, waits for them, and re-layouts: 4.48 us -> none  [the longest x4 2.53 us: one_block(): old = lax.dynamic_slice_in_dim(acc, first, block, 0)]
    slice x1 -> x0, local copies, waits for them, and re-layouts: 3.71 us -> none  [local(): values4 = piece[0, 1].reshape(length, HEADS, head)]
    ppermute x4 -> x2, starting transfers between devices: 1.02 us -> 4.71 us  [the longest x1 2.97 us: local(): lax.ppermute(cache, 'helper', [(i, (i + j) % helpers) for i in range(help...]
    select_n x3 -> x0, other arithmetic: 2.26 us -> none  [local(): tokens = jnp.where(offset >> level & 1 == 1, moved, tokens)]
  transfers between devices with their start and end apart: 5 -> 2, of which waited for: 4 -> 2; matrix products, arithmetic and copies ran while one was open for 13% -> 6% of each run, Pallas kernels for 0% -> 17%
where the time goes in v1:
time: 47.2 us; the launch traced here: 46.8 us
  waiting for transfers between devices  20.1 us (43%)
  Pallas kernels  15.2 us (32%)
  starting transfers between devices  4.71 us (10%)
  other arithmetic  2.55 us (5%)
  local copies, waits for them, and re-layouts  2.24 us (5%)
  between operations  2.02 us (4%)
    ppermute x1, waiting for transfers between devices, turn(): return lambda t: lax.ppermute(t, 'group', pairs) if s else t  19 us
    pallas_call x1, Pallas kernels, local(): pl.pallas_call(functools.partial(first_kernel, head, scale), grid=(steps,...  8.15 us
    pallas_call x1, Pallas kernels, local(): pl.pallas_call(functools.partial(last_kernel, head, scale, pieces), grid=...  7.06 us
    ppermute x1, starting transfers between devices, local(): lax.ppermute(cache, 'helper', [(i, (i + j) % helpers) for i in range(help...  2.97 us
    unnamed x3, local copies, waits for them, and re-layouts  2.21 us
    ppermute x1, starting transfers between devices, turn(): return lambda t: lax.ppermute(t, 'group', pairs) if s else t  1.74 us
    reduce_sum x1, other arithmetic, pick(): return jnp.sum(jnp.where(places == index, table, 0))  1.37 us
    another operation x1, other arithmetic, local(): info = jnp.stack([visible, live] + bases).astype(jnp.int32)  1.18 us
  transfers between devices with their start and end apart: 2, of which 2 were waited for; matrix products, arithmetic and copies ran while one was open for 6% of the time, Pallas kernels for 17%

profile of v1, /device:TPU:0, one launch (start us, length us, event | category | flops | bytes accessed | tf_op | source)
XLA Modules:
  0.0 46.8 jit_solution(8055663965339913930)
XLA Ops:
  0.0 1.0 %copy.26 = bf16[1,256,1024]{2,1,0:T(8,128)(2,1)S(1)} copy(bf16[1,256,1024]{2,1,0:T(8,128)(2,1)} %param.24) | data formatting | bytes 1048576
  1.0 3.0 %collective-permute-start.15 = (bf16[2,384,1024]{2,1,0:T(8,128)(2,1)}, bf16[2,384,1024]{2,1,0:T(8,128)(2,1)S(1)}, u32[]{:S(2)}, u32[]{:S(2)}) collective-permute-start(bf16[2,384,1024]{2,1,0:T(8,128)(2,1)} %bitcast.10), channel_id=1, source_target_pairs={{0,1},{1,0},{2,3},{3,2},{4,5},{5,4},{6,7},{7,6},{8,9},{9,8},{10,11... | collective-permute-start | bytes 4718600 | tf_op jit(solution)/shard_map/ppermute | solution.py:95
  5.3 1.4 %fusion = (s32[]{:T(128)}, s32[]{:T(128)}) fusion(s32[16]{0:T(128)} %param.31, s32[]{:T(128)S(6)} %select_n.22, s32[16]{0:T(128)} %param.30), kind=kLoop, calls=%fused_computation.2 | loop fusion | flops 78 | bytes 140 | tf_op jit(solution)/shard_map/reduce_sum | solution.py:17
  7.4 20.9 %conditional.1 = (bf16[256,1024]{1,0:T(8,128)(2,1)S(1)}) conditional(s32[]{:T(128)} %clamp.3, bf16[256,1024]{1,0:T(8,128)(2,1)S(1)} %bitcast.13, bf16[256,1024]{1,0:T(8,128)(2,1)S(1)} %bitcast.14, bf16[256,1024]{1,0:T(8,128)(2,1)S(1)} %bitcast.15, bf16[256,1024]{1,0:T(8,128)(2,1)S(1)} %bitcast.16, ...), branch_computations={%region_2.0_spmd, %region_3.0_spmd, %region_4.0_spmd, %region_5.0_... | conditional | bytes 3145776 | solution.py:103
  7.4 1.7 %collective-permute-start.6 = (bf16[256,1024]{1,0:T(8,128)(2,1)S(1)}, bf16[256,1024]{1,0:T(8,128)(2,1)S(1)}, u32[]{:S(2)}, u32[]{:S(2)}) collective-permute-start(bf16[256,1024]{1,0:T(8,128)(2,1)S(1)} %param.7), channel_id=1, source_target_pairs={{0,14},{2,16},{4,18},{6,20},{8,22},{10,24},{12,26},{14,28},{16,30}... | collective-permute-start | bytes 1572872 | tf_op jit(solution)/shard_map/cond/branch_7_fun/ppermute | solution.py:101
  9.2 19.0 %collective-permute-done.6 = bf16[256,1024]{1,0:T(8,128)(2,1)S(1)} collective-permute-done((bf16[256,1024]{1,0:T(8,128)(2,1)S(1)}, bf16[256,1024]{1,0:T(8,128)(2,1)S(1)}, u32[]{:S(2)}, u32[]{:S(2)}) %collective-permute-start.6) | collective-permute-done | bytes 524320 | tf_op jit(solution)/shard_map/cond/branch_7_fun/ppermute | solution.py:101
  28.3 1.2 %pad_add_fusion.info = s32[4]{0:T(128)} fusion(s32[1]{0:T(128)} %bitcast.4, s32[1]{0:T(128)} %bitcast.3, s32[1]{0:T(128)} %bitcast.2, s32[1]{0:T(128)} %bitcast.1), kind=kLoop, calls=%fused_computation.4 | loop fusion | flops 12 | bytes 32 | tf_op jit(solution)/shard_map/stack | solution.py:109
  29.5 8.1 %first.1 = (f32[256,1024]{1,0:T(8,128)}, bf16[256,1024]{1,0:T(8,128)(2,1)}, f32[256,1024]{1,0:T(8,128)}) custom-call(s32[4]{0:T(128)} %pad_add_fusion.info, bf16[256,1024]{1,0:T(8,128)(2,1)S(1)} %get-tuple-element.46.tok, bf16[1024,4096]{1,0:T(8,128)(2,1)} %wk.1, bf16[1024,4096]{1,0:T(8,128)(2,1)} %wk.1, bf16[1024,4096]{1,0:T(8,128)(2,1)} %wk.1, ...), custom_call_target="tpu_custom_call" | custom-call | flops 2550136832 | bytes 13107200 | tf_op jit(solution)/shard_map/first/pallas_call | solution.py:118
  37.6 1.0 %collective-permute-done.15.rest_0_.rest_1_ = bf16[2,384,1024]{2,1,0:T(8,128)(2,1)S(1)} collective-permute-done((bf16[2,384,1024]{2,1,0:T(8,128)(2,1)}, bf16[2,384,1024]{2,1,0:T(8,128)(2,1)S(1)}, u32[]{:S(2)}, u32[]{:S(2)}) %collective-permute-start.15) | collective-permute-done | bytes 1572896 | tf_op jit(solution)/shard_map/ppermute | solution.py:95
  38.6 0.0 copy-start
  38.6 1.2 %copy-done = bf16[2,384,1024]{2,1,0:T(8,128)(2,1)} copy-done((bf16[2,384,1024]{2,1,0:T(8,128)(2,1)}, bf16[2,384,1024]{2,1,0:T(8,128)(2,1)S(1)}, u32[]{:S(2)}) %copy-start) | copy-done | bytes 1572888
  39.8 7.1 %last.1 = bf16[256,1024]{1,0:T(8,128)(2,1)} custom-call(s32[4]{0:T(128)} %pad_add_fusion.info, bf16[256,1024]{1,0:T(8,128)(2,1)} %get-tuple-element.41.q, f32[256,1024]{1,0:T(8,128)} %get-tuple-element.42.acc, f32[256,1024]{1,0:T(8,128)} %get-tuple-element.43.u, f32[1,1024]{1,0:T(1,128)} %bitcast.29, bf16[1024,1024]{1,0:T(8,128)(2,1)} %w_out.1, ...), custom_call_target="tpu_custom_call" | custom-call | flops 939524096 | bytes 6815744 | tf_op jit(solution)/shard_map/last/pallas_call | solution.py:139
  (1 shorter events, 0.0 us)
Async XLA Ops:
  1.0 37.6 %collective-permute-start.15 = (bf16[2,384,1024]{2,1,0:T(8,128)(2,1)}, bf16[2,384,1024]{2,1,0:T(8,128)(2,1)S(1)}, u32[]{:S(2)}, u32[]{:S(2)}) collective-permute-start(bf16[2,384,1024]{2,1,0:T(8,128)(2,1)} %bitcast.10), channel_id=1, source_target_pairs={{0,1},{1,0},{2,3},{3,2},{4,5},{5,4},{6,7},{7,6},{8,9},{9,8},{10,11... | collective-permute-start | bytes 4718600 | tf_op jit(solution)/shard_map/ppermute | solution.py:95
  7.4 20.8 %collective-permute-start.6 = (bf16[256,1024]{1,0:T(8,128)(2,1)S(1)}, bf16[256,1024]{1,0:T(8,128)(2,1)S(1)}, u32[]{:S(2)}, u32[]{:S(2)}) collective-permute-start(bf16[256,1024]{1,0:T(8,128)(2,1)S(1)} %param.7), channel_id=1, source_target_pairs={{0,14},{2,16},{4,18},{6,20},{8,22},{10,24},{12,26},{14,28},{16,30}... | collective-permute-start | bytes 1572872 | tf_op jit(solution)/shard_map/cond/branch_7_fun/ppermute | solution.py:101
  38.6 1.2 %copy-start = (bf16[2,384,1024]{2,1,0:T(8,128)(2,1)}, bf16[2,384,1024]{2,1,0:T(8,128)(2,1)S(1)}, u32[]{:S(2)}) copy-start(bf16[2,384,1024]{2,1,0:T(8,128)(2,1)S(1)} %collective-permute-done.15.rest_0_.rest_1_) | copy-start | bytes 4718596

commit v2 on v1

v2 whole, which is shorter than its diff:
```python
import functools
import math

import jax
import jax.numpy as jnp
from jax import lax
from jax.experimental import pallas as pl
from jax.experimental.pallas import tpu as pltpu
from jax.sharding import PartitionSpec as P

HEADS = 8
EPS = 1e-05


def silu(v):
    t = v * 0.5
    return t + t * jnp.tanh(t)


def weigh(query, keys, scale):
    scores = lax.dot_general(
        query, keys, (((1,), (1,)), ((), ())), preferred_element_type=jnp.float32
    )
    t = scores * (0.5 * scale)
    return (t + t * jnp.tanh(t)).astype(jnp.bfloat16)


def user_here(owner):
    groups = lax.axis_size("group")
    return lax.rem(lax.axis_index("group") - owner[0] + groups, groups)


def piece_base(away, length):
    helpers = lax.axis_size("helper")
    return lax.rem(lax.axis_index("helper") - away + helpers, helpers) * length


def seen(values, base, visible):
    rows = lax.broadcasted_iota(jnp.int32, values.shape, 0) + base
    return jnp.where(rows < visible, values, jnp.zeros_like(values))


def first_kernel(head, scale, owner, prefix_len, tok, w, cache, u_out, q_out, acc_out):
    width = tok.shape[1]
    wide = 2 * head
    length = cache.shape[1]
    visible = prefix_len[user_here(owner)]
    base = piece_base(0, length)
    for pair in range(width // wide):
        cols = slice(pair * wide, (pair + 1) * wide)

        def project(k):
            at = slice(k * width + pair * wide, k * width + (pair + 1) * wide)
            return silu(jnp.dot(tok[...], w[:, at], preferred_element_type=jnp.float32))

        query = project(2).astype(jnp.bfloat16)
        q_out[:, cols] = query
        own_k = project(3).astype(jnp.bfloat16).astype(jnp.float32)
        own_v = project(1).astype(jnp.bfloat16).astype(jnp.float32)
        u_out[:, cols] = project(0)
        prod = query.astype(jnp.float32) * own_k
        values = seen(cache[1, :, cols], base, visible)
        for n in range(wide // head):
            here = slice(n * head, (n + 1) * head)
            at = slice(pair * wide + n * head, pair * wide + (n + 1) * head)
            selfw = silu(jnp.sum(prod[:, here], axis=1, keepdims=True) * scale)
            selfw = selfw.astype(jnp.bfloat16).astype(jnp.float32)
            weights = weigh(query[:, here], cache[0, :, at], scale)
            mixed = jnp.dot(weights, values[:, here], preferred_element_type=jnp.float32)
            acc_out[:, at] = mixed + selfw * own_v[:, here]


def weigh_kernel(head, scale, q, *refs):
    pieces = len(refs) // 2
    for p in range(pieces):
        for n in range(q.shape[1] // head):
            at = slice(n * head, (n + 1) * head)
            refs[pieces + p][n] = weigh(q[:, at], refs[p][:, at], scale)


def last_kernel(head, pieces, owner, counts, prefix_len, acc, u, gain, w_out, *refs):
    weights, values, out, total = refs[:pieces], refs[pieces : 2 * pieces], refs[-2], refs[-1]
    slots, width = acc.shape
    user = user_here(owner)
    visible = prefix_len[user]
    live = counts[user] - lax.axis_index("helper") * slots
    for n in range(width // head):
        at = slice(n * head, (n + 1) * head)
        mixed = acc[:, at]
        for p in range(pieces):
            part = seen(values[p][:, at], piece_base(p + 1, values[p].shape[0]), visible)
            mixed += jnp.dot(weights[p][n], part, preferred_element_type=jnp.float32)
        total[:, at] = mixed
    block = math.gcd(slots, 128)
    for first in range(0, slots, block):
        rows = slice(first, first + block)
        a = total[rows, :]
        centre = a - jnp.mean(a, axis=-1, keepdims=True)
        spread = jnp.mean(centre * centre, axis=-1, keepdims=True)
        normed = (centre * lax.rsqrt(spread + EPS) * gain[...] * u[rows, :]).astype(jnp.bfloat16)
        result = jnp.dot(normed, w_out[...], preferred_element_type=jnp.float32)
        places = lax.broadcasted_iota(jnp.int32, result.shape, 0) + first
        out[rows, :] = jnp.where(places < live, result, 0.0).astype(jnp.bfloat16)


def local(candidates, prefix_cache, w_uvqk, w_output, norm_gain, owner, counts, prefix_len):
    groups = lax.axis_size("group")
    helpers = lax.axis_size("helper")
    _, slots, width = candidates.shape
    length = prefix_cache.shape[2]
    head = width // HEADS
    scale = head ** (-0.5)
    cache = prefix_cache.reshape(2, length, width)
    pieces = helpers - 1

    def from_helper(value, away):
        pairs = [(i, (i + away) % helpers) for i in range(helpers)]
        return lax.ppermute(value, "helper", pairs)

    keys = [from_helper(cache[0], away) for away in range(1, helpers)]
    values = [from_helper(cache[1], away) for away in range(1, helpers)]

    def turn(s):
        pairs = [(i, (i + s) % groups) for i in range(groups)]
        return lambda t: lax.ppermute(t, "group", pairs) if s else t

    tokens = lax.switch(owner[0], [turn(s) for s in range(groups)], candidates[0])

    smem = pl.BlockSpec(memory_space=pltpu.SMEM)
    vmem = pl.BlockSpec(memory_space=pltpu.VMEM)
    params = pltpu.CompilerParams(vmem_limit_bytes=28 * 1024 * 1024)
    rows = lambda kind: jax.ShapeDtypeStruct((slots, width), kind)
    gate_u, query, acc = pl.pallas_call(
        functools.partial(first_kernel, head, scale),
        in_specs=[smem, smem, vmem, vmem, vmem],
        out_specs=[vmem] * 3,
        out_shape=[rows(jnp.float32), rows(jnp.bfloat16), rows(jnp.float32)],
        cost_estimate=pl.CostEstimate(
            flops=2 * slots * width * (4 * width + 2 * length),
            bytes_accessed=8 * width * width + 4 * length * width + 12 * slots * width,
            transcendentals=slots * (4 * width + HEADS * length),
        ),
        compiler_params=params,
        name="first",
    )(owner, prefix_len, tokens, w_uvqk, cache)
    weights = pl.pallas_call(
        functools.partial(weigh_kernel, head, scale),
        in_specs=[vmem] * (1 + pieces),
        out_specs=[vmem] * pieces,
        out_shape=[jax.ShapeDtypeStruct((HEADS, slots, length), jnp.bfloat16)] * pieces,
        cost_estimate=pl.CostEstimate(
            flops=2 * slots * width * length * pieces,
            bytes_accessed=2 * length * width * pieces,
            transcendentals=slots * HEADS * length * pieces,
        ),
        compiler_params=params,
        name="weigh",
    )(query, *keys)
    result = pl.pallas_call(
        functools.partial(last_kernel, head, pieces),
        in_specs=[smem] * 3 + [vmem] * (4 + 2 * pieces),
        out_specs=vmem,
        out_shape=rows(jnp.bfloat16),
        scratch_shapes=[pltpu.VMEM((slots, width), jnp.float32)],
        cost_estimate=pl.CostEstimate(
            flops=2 * slots * width * (width + length * pieces),
            bytes_accessed=2 * width * width + 2 * length * width * pieces,
            transcendentals=slots,
        ),
        compiler_params=params,
        name="last",
    )(owner, counts, prefix_len, acc, gate_u, norm_gain.reshape(1, width), w_output, *weights, *values)
    return result[None]


def solution(mesh):
    in_specs = (
        P("group", "helper", None),
        P("group", None, "helper", None),
        P(),
        P(),
        P(),
        P(),
        P(),
        P(),
    )
    out_specs = P("group", "helper", None)
    return jax.shard_map(local, mesh=mesh, in_specs=in_specs, out_specs=out_specs, check_vma=False)
```

time: 47.2 us -> 45.4 us (0.962)
  local copies, waits for them, and re-layouts: 2.24 us -> 8.76 us
  Pallas kernels: 15.2 us -> 9.47 us
  waiting for transfers between devices: 20.1 us -> 22.8 us
  other arithmetic: 2.55 us -> 0 us
  between operations: 2.02 us -> 0.12 us
  starting transfers between devices: 4.71 us -> 3.95 us
    ppermute x1 -> x2, waiting for transfers between devices: 1 us -> 13.1 us  [from_helper(): return lax.ppermute(value, 'helper', pairs)]
    ppermute x1, waiting for transfers between devices: 19 us -> 9.71 us  [turn(): return lambda t: lax.ppermute(t, 'group', pairs) if s else t]
    pallas_call x2 -> x3, Pallas kernels: 15.2 us -> 9.47 us  [the longest x1 5.56 us: local(): pl.pallas_call(functools.partial(first_kernel, head, scale), in_specs=[sm...]
    unnamed x3 -> x15, local copies, waits for them, and re-layouts: 2.21 us -> 5.28 us
    squeeze x0 -> x1, local copies, waits for them, and re-layouts: none -> 2.68 us  [local(): values = [from_helper(cache[1], away) for away in range(1, helpers)]]
    reduce_sum x1 -> x0, other arithmetic: 1.37 us -> none  [pick(): return jnp.sum(jnp.where(places == index, table, 0))]
    another operation x1 -> x0, other arithmetic: 1.18 us -> none  [local(): info = jnp.stack([visible, live] + bases).astype(jnp.int32)]
    ppermute x1, starting transfers between devices: 1.74 us -> 0.96 us  [turn(): return lambda t: lax.ppermute(t, 'group', pairs) if s else t]
  transfers between devices with their start and end apart: 2 -> 3, of which waited for: 2 -> 2; matrix products, arithmetic and copies ran while one was open for 6% -> 2% of each run, Pallas kernels for 17% -> 14%
where the time goes in v2:
time: 45.4 us; the launch traced here: 45.1 us
  waiting for transfers between devices  22.8 us (50%)
  Pallas kernels  9.47 us (21%)
  local copies, waits for them, and re-layouts  8.76 us (19%)
  starting transfers between devices  3.95 us (9%)
    ppermute x2, waiting for transfers between devices, from_helper(): return lax.ppermute(value, 'helper', pairs)  13.1 us
    ppermute x1, waiting for transfers between devices, turn(): return lambda t: lax.ppermute(t, 'group', pairs) if s else t  9.71 us
    pallas_call x1, Pallas kernels, local(): pl.pallas_call(functools.partial(first_kernel, head, scale), in_specs=[sm...  5.56 us
    unnamed x15, local copies, waits for them, and re-layouts  5.28 us
    pallas_call x1, Pallas kernels, local(): pl.pallas_call(functools.partial(last_kernel, head, pieces), in_specs=[sm...  3 us
    ppermute x2, starting transfers between devices, from_helper(): return lax.ppermute(value, 'helper', pairs)  2.99 us
    squeeze x1, local copies, waits for them, and re-layouts, local(): values = [from_helper(cache[1], away) for away in range(1, helpers)]  2.68 us
    ppermute x1, starting transfers between devices, turn(): return lambda t: lax.ppermute(t, 'group', pairs) if s else t  0.96 us
  transfers between devices with their start and end apart: 3, of which 2 were waited for; matrix products, arithmetic and copies ran while one was open for 2% of the time, Pallas kernels for 14%

profile of v2, /device:TPU:0, one launch (start us, length us, event | category | flops | bytes accessed | tf_op | source)
XLA Modules:
  0.0 45.1 jit_solution(9380703810606994401)
XLA Ops:
  0.0 1.9 %copy.26 = bf16[1,256,1024]{2,1,0:T(8,128)(2,1)} copy(bf16[1,256,1024]{2,1,0:T(8,128)(2,1)} %param.24) | data formatting | bytes 1048576
  1.9 0.0 copy-start.3
  1.9 2.7 %slice_bitcast_fusion = (bf16[384,1024]{1,0:T(8,128)(2,1)}, bf16[384,1024]{1,0:T(8,128)(2,1)}) fusion(bf16[1,2,384,1024]{3,2,1,0:T(8,128)(2,1)} %param.25), kind=kLoop, calls=%fused_computation | loop fusion | bytes 3145728 | tf_op jit(solution)/shard_map/squeeze | solution.py:121
  4.6 3.0 %collective-permute-start.15 = (bf16[384,1024]{1,0:T(8,128)(2,1)}, bf16[384,1024]{1,0:T(8,128)(2,1)S(1)}, u32[]{:S(2)}, u32[]{:S(2)}) collective-permute-start(bf16[384,1024]{1,0:T(8,128)(2,1)} %get-tuple-element.45), channel_id=1, source_target_pairs={{0,1},{1,0},{2,3},{3,2},{4,5},{5,4},{6,7},{7,6},{8,9},{9,8},{10,11... | collective-permute-start | bytes 2359304 | tf_op jit(solution)/shard_map/ppermute | solution.py:118
  7.5 0.0 collective-permute-start.16
  7.5 0.0 copy-done.3
  7.6 0.0 copy-start.1
  7.6 0.0 copy-start.5
  7.6 11.5 %conditional.1 = (bf16[256,1024]{1,0:T(8,128)(2,1)}) conditional(s32[]{:T(128)} %bitcast, bf16[256,1024]{1,0:T(8,128)(2,1)} %bitcast.13, bf16[256,1024]{1,0:T(8,128)(2,1)} %bitcast.14, bf16[256,1024]{1,0:T(8,128)(2,1)} %bitcast.15, bf16[256,1024]{1,0:T(8,128)(2,1)} %bitcast.16, ...), branch_computations={%region_0.0_spmd, %region_1.0_spmd, %region_2.0_spmd, %region_3.0_... | conditional | bytes 3145776 | solution.py:127
  7.7 1.0 %collective-permute-start.2 = (bf16[256,1024]{1,0:T(8,128)(2,1)}, bf16[256,1024]{1,0:T(8,128)(2,1)S(1)}, u32[]{:S(2)}, u32[]{:S(2)}) collective-permute-start(bf16[256,1024]{1,0:T(8,128)(2,1)} %param.3), channel_id=1, source_target_pairs={{0,6},{2,8},{4,10},{6,12},{8,14},{10,16},{12,18},{14,20},{16,22},{... | collective-permute-start | bytes 1572872 | tf_op jit(solution)/shard_map/cond/branch_3_fun/ppermute | solution.py:125
  8.6 9.7 %collective-permute-done.2 = bf16[256,1024]{1,0:T(8,128)(2,1)S(1)} collective-permute-done((bf16[256,1024]{1,0:T(8,128)(2,1)}, bf16[256,1024]{1,0:T(8,128)(2,1)S(1)}, u32[]{:S(2)}, u32[]{:S(2)}) %collective-permute-start.2) | collective-permute-done | bytes 524320 | tf_op jit(solution)/shard_map/cond/branch_3_fun/ppermute | solution.py:125
  18.3 0.8 %copy.12 = bf16[256,1024]{1,0:T(8,128)(2,1)} copy(bf16[256,1024]{1,0:T(8,128)(2,1)S(1)} %collective-permute-done.2) | data formatting | bytes 1048576 | tf_op jit(solution)/shard_map/cond
  19.1 0.0 copy-done.1
  19.1 0.0 copy-done.5
  19.1 0.0 copy-start
  19.1 3.4 %copy-done = bf16[1024,4096]{1,0:T(8,128)(2,1)S(1)} copy-done((bf16[1024,4096]{1,0:T(8,128)(2,1)S(1)}, bf16[1024,4096]{1,0:T(8,128)(2,1)}, u32[]{:S(2)}) %copy-start) | copy-done | bytes 8388632
  22.5 5.6 %first.1 = (f32[256,1024]{1,0:T(8,128)S(1)}, bf16[256,1024]{1,0:T(8,128)(2,1)S(1)}, f32[256,1024]{1,0:T(8,128)S(1)}) custom-call(s32[16]{0:T(128)S(1)} %copy-done.3, s32[16]{0:T(128)S(1)} %copy-done.5, bf16[256,1024]{1,0:T(8,128)(2,1)} %get-tuple-element.46.tok, bf16[1024,4096]{1,0:T(8,128)(2,1)S(1)} %copy-done, bf16[2,384,1024]{2,1,0:T(8,128)(2,1)S(1)} %bitcast.10), custom_call_target="tpu_custom_call" | custom-call | flops 2550136832 | bytes 13107200 | tf_op jit(solution)/shard_map/first/pallas_call | solution.py:133
  28.1 0.0 copy-start.2
  28.1 0.0 copy-start.4
  28.1 0.0 copy-start.6
  28.1 0.0 collective-permute-done.15.refs_0_
  28.1 0.9 %weigh.1.refs_0_ = bf16[8,256,384]{2,1,0:T(8,128)(2,1)S(1)} custom-call(bf16[256,1024]{1,0:T(8,128)(2,1)S(1)} %get-tuple-element.43.q, bf16[384,1024]{1,0:T(8,128)(2,1)S(1)} %collective-permute-done.15.refs_0_), custom_call_target="tpu_custom_call" | custom-call | flops 201326592 | bytes 786432 | tf_op jit(solution)/shard_map/weigh/pallas_call | solution.py:146
  29.0 13.1 %collective-permute-done.16.refs_1_ = bf16[384,1024]{1,0:T(8,128)(2,1)S(1)} collective-permute-done((bf16[384,1024]{1,0:T(8,128)(2,1)}, bf16[384,1024]{1,0:T(8,128)(2,1)S(1)}, u32[]{:S(2)}, u32[]{:S(2)}) %collective-permute-start.16) | collective-permute-done | bytes 786464 | tf_op jit(solution)/shard_map/ppermute | solution.py:118
  42.1 0.0 copy-done.2
  42.1 0.0 copy-done.4
  42.1 0.0 copy-done.6
  42.1 3.0 %last.1 = bf16[256,1024]{1,0:T(8,128)(2,1)} custom-call(s32[16]{0:T(128)S(1)} %copy-done.3, s32[16]{0:T(128)S(1)} %copy-done.6, s32[16]{0:T(128)S(1)} %copy-done.5, f32[256,1024]{1,0:T(8,128)S(1)} %get-tuple-element.41.acc, f32[256,1024]{1,0:T(8,128)S(1)} %get-tuple-element.42.u, f32[1,1024]{1,0:T(1,128)S(1)} %bitcast.12, bf16[1024,1024]{1,0:T(8,128)(2,1)S(1)} %copy-done.2, ...), custom_call_target="tpu_custom_call" | custom-call | flops 738197504 | bytes 2883584 | tf_op jit(solution)/shard_map/last/pallas_call | solution.py:159
Async XLA Ops:
  1.9 5.7 %copy-start.3 = (s32[16]{0:T(128)S(1)}, s32[16]{0:T(128)}, u32[]{:S(2)}) copy-start(s32[16]{0:T(128)} %owner.3) | copy-start | bytes 196
  4.6 23.6 %collective-permute-start.15 = (bf16[384,1024]{1,0:T(8,128)(2,1)}, bf16[384,1024]{1,0:T(8,128)(2,1)S(1)}, u32[]{:S(2)}, u32[]{:S(2)}) collective-permute-start(bf16[384,1024]{1,0:T(8,128)(2,1)} %get-tuple-element.45), channel_id=1, source_target_pairs={{0,1},{1,0},{2,3},{3,2},{4,5},{5,4},{6,7},{7,6},{8,9},{9,8},{10,11... | collective-permute-start | bytes 2359304 | tf_op jit(solution)/shard_map/ppermute | solution.py:118
  7.5 34.6 %collective-permute-start.16 = (bf16[384,1024]{1,0:T(8,128)(2,1)}, bf16[384,1024]{1,0:T(8,128)(2,1)S(1)}, u32[]{:S(2)}, u32[]{:S(2)}) collective-permute-start(bf16[384,1024]{1,0:T(8,128)(2,1)} %get-tuple-element.44), channel_id=1, source_target_pairs={{0,1},{1,0},{2,3},{3,2},{4,5},{5,4},{6,7},{7,6},{8,9},{9,8},{10,11... | collective-permute-start | bytes 2359304 | tf_op jit(solution)/shard_map/ppermute | solution.py:118
  7.6 11.5 %copy-start.1 = (bf16[1,2,384,1024]{3,2,1,0:T(8,128)(2,1)S(1)}, bf16[1,2,384,1024]{3,2,1,0:T(8,128)(2,1)}, u32[]{:S(2)}) copy-start(bf16[1,2,384,1024]{3,2,1,0:T(8,128)(2,1)} %param.25) | copy-start | bytes 4718596
  7.6 11.5 %copy-start.5 = (s32[16]{0:T(128)S(1)}, s32[16]{0:T(128)}, u32[]{:S(2)}) copy-start(s32[16]{0:T(128)} %prefix_len.3) | copy-start | bytes 196
  7.7 10.7 %collective-permute-start.2 = (bf16[256,1024]{1,0:T(8,128)(2,1)}, bf16[256,1024]{1,0:T(8,128)(2,1)S(1)}, u32[]{:S(2)}, u32[]{:S(2)}) collective-permute-start(bf16[256,1024]{1,0:T(8,128)(2,1)} %param.3), channel_id=1, source_target_pairs={{0,6},{2,8},{4,10},{6,12},{8,14},{10,16},{12,18},{14,20},{16,22},{... | collective-permute-start | bytes 1572872 | tf_op jit(solution)/shard_map/cond/branch_3_fun/ppermute | solution.py:125
  19.1 3.4 %copy-start = (bf16[1024,4096]{1,0:T(8,128)(2,1)S(1)}, bf16[1024,4096]{1,0:T(8,128)(2,1)}, u32[]{:S(2)}) copy-start(bf16[1024,4096]{1,0:T(8,128)(2,1)} %w.1) | copy-start | bytes 25165828
  28.1 14.0 %copy-start.2 = (bf16[1024,1024]{1,0:T(8,128)(2,1)S(1)}, bf16[1024,1024]{1,0:T(8,128)(2,1)}, u32[]{:S(2)}) copy-start(bf16[1024,1024]{1,0:T(8,128)(2,1)} %w_out.1) | copy-start | bytes 6291460
  28.1 14.0 %copy-start.4 = (f32[1024]{0:T(1024)S(1)}, f32[1024]{0:T(1024)}, u32[]{:S(2)}) copy-start(f32[1024]{0:T(1024)} %param.28) | copy-start | bytes 12292
  28.1 14.0 %copy-start.6 = (s32[16]{0:T(128)S(1)}, s32[16]{0:T(128)}, u32[]{:S(2)}) copy-start(s32[16]{0:T(128)} %counts.1) | copy-start | bytes 196

commit v3 on v2

--- a/solution.py
+++ b/solution.py
@@ -70,37 +70,38 @@
             acc_out[:, at] = mixed + selfw * own_v[:, here]
 
 
-def weigh_kernel(head, scale, q, *refs):
-    pieces = len(refs) // 2
-    for p in range(pieces):
-        for n in range(q.shape[1] // head):
-            at = slice(n * head, (n + 1) * head)
-            refs[pieces + p][n] = weigh(q[:, at], refs[p][:, at], scale)
-
-
-def last_kernel(head, pieces, owner, counts, prefix_len, acc, u, gain, w_out, *refs):
-    weights, values, out, total = refs[:pieces], refs[pieces : 2 * pieces], refs[-2], refs[-1]
+def last_kernel(head, scale, pieces, owner, counts, prefix_len, q, acc, u, gain, w_out, *refs):
+    caches, out, values, total, staged, sems = refs[:pieces], *refs[pieces:]
     slots, width = acc.shape
+    length = caches[0].shape[1]
     user = user_here(owner)
     visible = prefix_len[user]
     live = counts[user] - lax.axis_index("helper") * slots
-    for n in range(width // head):
-        at = slice(n * head, (n + 1) * head)
-        mixed = acc[:, at]
-        for p in range(pieces):
-            part = seen(values[p][:, at], piece_base(p + 1, values[p].shape[0]), visible)
-            mixed += jnp.dot(weights[p][n], part, preferred_element_type=jnp.float32)
-        total[:, at] = mixed
+    for p in range(pieces):
+        values[p] = seen(caches[p][1], piece_base(p + 1, length), visible)
     block = math.gcd(slots, 128)
+    copies = []
     for first in range(0, slots, block):
         rows = slice(first, first + block)
+        for n in range(width // head):
+            at = slice(n * head, (n + 1) * head)
+            mixed = acc[rows, at]
+            for p in range(pieces):
+                weights = weigh(q[rows, at], caches[p][0, :, at], scale)
+                mixed += jnp.dot(weights, values[p, :, at], preferred_element_type=jnp.float32)
+            total[rows, at] = mixed
         a = total[rows, :]
         centre = a - jnp.mean(a, axis=-1, keepdims=True)
         spread = jnp.mean(centre * centre, axis=-1, keepdims=True)
         normed = (centre * lax.rsqrt(spread + EPS) * gain[...] * u[rows, :]).astype(jnp.bfloat16)
         result = jnp.dot(normed, w_out[...], preferred_element_type=jnp.float32)
         places = lax.broadcasted_iota(jnp.int32, result.shape, 0) + first
-        out[rows, :] = jnp.where(places < live, result, 0.0).astype(jnp.bfloat16)
+        staged[rows, :] = jnp.where(places < live, result, 0.0).astype(jnp.bfloat16)
+        copy = pltpu.make_async_copy(staged.at[rows], out.at[rows], sems.at[first // block])
+        copy.start()
+        copies.append(copy)
+    for copy in copies:
+        copy.wait()
 
 
 def local(candidates, prefix_cache, w_uvqk, w_output, norm_gain, owner, counts, prefix_len):
@@ -117,12 +118,11 @@
         pairs = [(i, (i + away) % helpers) for i in range(helpers)]
         return lax.ppermute(value, "helper", pairs)
 
-    keys = [from_helper(cache[0], away) for away in range(1, helpers)]
-    values = [from_helper(cache[1], away) for away in range(1, helpers)]
+    got = [from_helper(cache, away) for away in range(1, helpers)]
 
     def turn(s):
         pairs = [(i, (i + s) % groups) for i in range(groups)]
-        return lambda t: lax.ppermute(t, "group", pairs) if s else t
+        return lambda t: lax.ppermute(t, "group", pairs)
 
     tokens = lax.switch(owner[0], [turn(s) for s in range(groups)], candidates[0])
 
@@ -143,33 +143,25 @@
         compiler_params=params,
         name="first",
     )(owner, prefix_len, tokens, w_uvqk, cache)
-    weights = pl.pallas_call(
-        functools.partial(weigh_kernel, head, scale),
-        in_specs=[vmem] * (1 + pieces),
-        out_specs=[vmem] * pieces,
-        out_shape=[jax.ShapeDtypeStruct((HEADS, slots, length), jnp.bfloat16)] * pieces,
+    result = pl.pallas_call(
+        functools.partial(last_kernel, head, scale, pieces),
+        in_specs=[smem] * 3 + [vmem] * (5 + pieces),
+        out_specs=pl.BlockSpec(memory_space=pl.ANY),
+        out_shape=rows(jnp.bfloat16),
+        scratch_shapes=[
+            pltpu.VMEM((pieces, length, width), jnp.bfloat16),
+            pltpu.VMEM((slots, width), jnp.float32),
+            pltpu.VMEM((slots, width), jnp.bfloat16),
+            pltpu.SemaphoreType.DMA((slots // math.gcd(slots, 128),)),
+        ],
         cost_estimate=pl.CostEstimate(
-            flops=2 * slots * width * length * pieces,
-            bytes_accessed=2 * length * width * pieces,
+            flops=2 * slots * width * (width + 2 * length * pieces),
+            bytes_accessed=2 * width * width + 4 * length * width * pieces,
             transcendentals=slots * HEADS * length * pieces,
         ),
         compiler_params=params,
-        name="weigh",
-    )(query, *keys)
-    result = pl.pallas_call(
-        functools.partial(last_kernel, head, pieces),
-        in_specs=[smem] * 3 + [vmem] * (4 + 2 * pieces),
-        out_specs=vmem,
-        out_shape=rows(jnp.bfloat16),
-        scratch_shapes=[pltpu.VMEM((slots, width), jnp.float32)],
-        cost_estimate=pl.CostEstimate(
-            flops=2 * slots * width * (width + length * pieces),
-            bytes_accessed=2 * width * width + 2 * length * width * pieces,
-            transcendentals=slots,
-        ),
-        compiler_params=params,
         name="last",
-    )(owner, counts, prefix_len, acc, gate_u, norm_gain.reshape(1, width), w_output, *weights, *values)
+    )(owner, counts, prefix_len, query, acc, gate_u, norm_gain.reshape(1, width), w_output, *got)
     return result[None]
 
 

time: 45.4 us -> 43.2 us (0.952)
  local copies, waits for them, and re-layouts: 8.76 us -> 6.11 us
  Pallas kernels: 9.47 us -> 11 us
  waiting for transfers between devices: 22.8 us -> 21.4 us
  between operations: 0.12 us -> 0.67 us
    ppermute x2 -> x1, waiting for transfers between devices: 13.1 us -> 0.16 us  [from_helper(): return lax.ppermute(value, 'helper', pairs)]
    ppermute x1, waiting for transfers between devices: 9.71 us -> 21.2 us  [turn(): return lambda t: lax.ppermute(t, 'group', pairs)]
    squeeze x1 -> x0, local copies, waits for them, and re-layouts: 2.68 us -> none  [local(): values = [from_helper(cache[1], away) for away in range(1, helpers)]]
    pallas_call x2 -> x1, Pallas kernels: 3.91 us -> 5.38 us  [local(): pl.pallas_call(functools.partial(last_kernel, head, scale, pieces), in_sp...]
    unnamed x15 -> x14, local copies, waits for them, and re-layouts: 5.28 us -> 6.11 us
    cond x1 -> x0, local copies, waits for them, and re-layouts: 0.79 us -> none
    ppermute x2 -> x1, starting transfers between devices: 2.99 us -> 2.97 us  [from_helper(): return lax.ppermute(value, 'helper', pairs)]
  transfers between devices with their start and end apart: 3 -> 2, of which waited for: 2 -> 2; matrix products, arithmetic and copies ran while one was open for 2% -> 0% of each run, Pallas kernels for 14% -> 13%
where the time goes in v3:
time: 43.2 us; the launch traced here: 43 us
  waiting for transfers between devices  21.4 us (50%)
  Pallas kernels  11 us (25%)
  local copies, waits for them, and re-layouts  6.11 us (14%)
  starting transfers between devices  3.76 us (9%)
  between operations  0.67 us (2%)
    ppermute x1, waiting for transfers between devices, turn(): return lambda t: lax.ppermute(t, 'group', pairs)  21.2 us
    unnamed x14, local copies, waits for them, and re-layouts  6.11 us
    pallas_call x1, Pallas kernels, local(): pl.pallas_call(functools.partial(first_kernel, head, scale), in_specs=[sm...  5.64 us
    pallas_call x1, Pallas kernels, local(): pl.pallas_call(functools.partial(last_kernel, head, scale, pieces), in_sp...  5.38 us
    ppermute x1, starting transfers between devices, from_helper(): return lax.ppermute(value, 'helper', pairs)  2.97 us
  transfers between devices with their start and end apart: 2, of which 2 were waited for; matrix products, arithmetic and copies ran while one was open for 0% of the time, Pallas kernels for 13%

profile of v3, /device:TPU:0, one launch (start us, length us, event | category | flops | bytes accessed | tf_op | source)
XLA Modules:
  0.0 43.0 jit_solution(14167260740293564999)
XLA Ops:
  0.0 3.0 %collective-permute-start.16 = (bf16[2,384,1024]{2,1,0:T(8,128)(2,1)}, bf16[2,384,1024]{2,1,0:T(8,128)(2,1)S(1)}, u32[]{:S(2)}, u32[]{:S(2)}) collective-permute-start(bf16[2,384,1024]{2,1,0:T(8,128)(2,1)} %bitcast.6), channel_id=1, source_target_pairs={{0,1},{1,0},{2,3},{3,2},{4,5},{5,4},{6,7},{7,6},{8,9},{9,8},{10,11... | collective-permute-start | bytes 4718600 | tf_op jit(solution)/shard_map/ppermute | solution.py:119
  3.6 22.0 %conditional.1 = (bf16[256,1024]{1,0:T(8,128)(2,1)}) conditional(s32[]{:T(128)} %bitcast, bf16[256,1024]{1,0:T(8,128)(2,1)} %bitcast.10, bf16[256,1024]{1,0:T(8,128)(2,1)} %bitcast.11, bf16[256,1024]{1,0:T(8,128)(2,1)} %bitcast.12, bf16[256,1024]{1,0:T(8,128)(2,1)} %bitcast.13, ...), branch_computations={%region_0.0_spmd, %region_1.0_spmd, %region_2.0_spmd, %region_3.0_... | conditional | bytes 2097200 | solution.py:127
  3.6 0.8 %collective-permute-start.5 = (bf16[256,1024]{1,0:T(8,128)(2,1)}, bf16[256,1024]{1,0:T(8,128)(2,1)}, u32[]{:S(2)}, u32[]{:S(2)}) collective-permute-start(bf16[256,1024]{1,0:T(8,128)(2,1)} %param.5), channel_id=1, source_target_pairs={{0,10},{2,12},{4,14},{6,16},{8,18},{10,20},{12,22},{14,24},{16,26}... | collective-permute-start | bytes 1572872 | tf_op jit(solution)/shard_map/cond/branch_5_fun/ppermute | solution.py:125
  4.4 21.2 %collective-permute-done.5 = bf16[256,1024]{1,0:T(8,128)(2,1)} collective-permute-done((bf16[256,1024]{1,0:T(8,128)(2,1)}, bf16[256,1024]{1,0:T(8,128)(2,1)}, u32[]{:S(2)}, u32[]{:S(2)}) %collective-permute-start.5) | collective-permute-done | bytes 524320 | tf_op jit(solution)/shard_map/cond/branch_5_fun/ppermute | solution.py:125
  25.7 0.0 copy-start
  25.7 3.4 %copy-done = bf16[1024,4096]{1,0:T(8,128)(2,1)S(1)} copy-done((bf16[1024,4096]{1,0:T(8,128)(2,1)S(1)}, bf16[1024,4096]{1,0:T(8,128)(2,1)}, u32[]{:S(2)}) %copy-start) | copy-done | bytes 8388632
  29.0 0.0 copy-start.2
  29.0 1.4 %copy-done.2 = bf16[1,2,384,1024]{3,2,1,0:T(8,128)(2,1)S(1)} copy-done((bf16[1,2,384,1024]{3,2,1,0:T(8,128)(2,1)S(1)}, bf16[1,2,384,1024]{3,2,1,0:T(8,128)(2,1)}, u32[]{:S(2)}) %copy-start.2) | copy-done | bytes 1572888
  30.4 0.0 copy-start.3
  30.4 0.7 %copy-done.3 = s32[16]{0:T(128)S(1)} copy-done((s32[16]{0:T(128)S(1)}, s32[16]{0:T(128)}, u32[]{:S(2)}) %copy-start.3) | copy-done | bytes 88
  31.1 0.0 copy-start.5
  31.1 0.7 %copy-done.5 = s32[16]{0:T(128)S(1)} copy-done((s32[16]{0:T(128)S(1)}, s32[16]{0:T(128)}, u32[]{:S(2)}) %copy-start.5) | copy-done | bytes 88
  31.8 0.0 copy-start.1
  31.8 0.0 copy-start.4
  31.8 0.0 copy-start.6
  31.8 5.6 %first.1 = (f32[256,1024]{1,0:T(8,128)S(1)}, bf16[256,1024]{1,0:T(8,128)(2,1)S(1)}, f32[256,1024]{1,0:T(8,128)S(1)}) custom-call(s32[16]{0:T(128)S(1)} %copy-done.3, s32[16]{0:T(128)S(1)} %copy-done.5, bf16[256,1024]{1,0:T(8,128)(2,1)} %get-tuple-element.44.tok, bf16[1024,4096]{1,0:T(8,128)(2,1)S(1)} %copy-done, bf16[2,384,1024]{2,1,0:T(8,128)(2,1)S(1)} %bitcast.7), custom_call_target="tpu_custom_call" | custom-call | flops 2550136832 | bytes 13107200 | tf_op jit(solution)/shard_map/first/pallas_call | solution.py:133
  37.4 0.2 collective-permute-done.16.refs_0_
  37.6 0.0 copy-done.1
  37.6 0.0 copy-done.4
  37.6 0.0 copy-done.6
  37.6 5.4 %last.1 = bf16[256,1024]{1,0:T(8,128)(2,1)} custom-call(s32[16]{0:T(128)S(1)} %copy-done.3, s32[16]{0:T(128)S(1)} %copy-done.6, s32[16]{0:T(128)S(1)} %copy-done.5, bf16[256,1024]{1,0:T(8,128)(2,1)S(1)} %get-tuple-element.41.q, f32[256,1024]{1,0:T(8,128)S(1)} %get-tuple-element.42.acc, f32[256,1024]{1,0:T(8,128)S(1)} %get-tuple-element.43.u, ...), custom_call_target="tpu_custom_call" | custom-call | flops 939524096 | bytes 3670016 | tf_op jit(solution)/shard_map/last/pallas_call | solution.py:146
Async XLA Ops:
  0.0 37.6 %collective-permute-start.16 = (bf16[2,384,1024]{2,1,0:T(8,128)(2,1)}, bf16[2,384,1024]{2,1,0:T(8,128)(2,1)S(1)}, u32[]{:S(2)}, u32[]{:S(2)}) collective-permute-start(bf16[2,384,1024]{2,1,0:T(8,128)(2,1)} %bitcast.6), channel_id=1, source_target_pairs={{0,1},{1,0},{2,3},{3,2},{4,5},{5,4},{6,7},{7,6},{8,9},{9,8},{10,11... | collective-permute-start | bytes 4718600 | tf_op jit(solution)/shard_map/ppermute | solution.py:119
  3.6 22.0 %collective-permute-start.5 = (bf16[256,1024]{1,0:T(8,128)(2,1)}, bf16[256,1024]{1,0:T(8,128)(2,1)}, u32[]{:S(2)}, u32[]{:S(2)}) collective-permute-start(bf16[256,1024]{1,0:T(8,128)(2,1)} %param.5), channel_id=1, source_target_pairs={{0,10},{2,12},{4,14},{6,16},{8,18},{10,20},{12,22},{14,24},{16,26}... | collective-permute-start | bytes 1572872 | tf_op jit(solution)/shard_map/cond/branch_5_fun/ppermute | solution.py:125
  25.7 3.4 %copy-start = (bf16[1024,4096]{1,0:T(8,128)(2,1)S(1)}, bf16[1024,4096]{1,0:T(8,128)(2,1)}, u32[]{:S(2)}) copy-start(bf16[1024,4096]{1,0:T(8,128)(2,1)} %w.1) | copy-start | bytes 25165828
  29.0 1.4 %copy-start.2 = (bf16[1,2,384,1024]{3,2,1,0:T(8,128)(2,1)S(1)}, bf16[1,2,384,1024]{3,2,1,0:T(8,128)(2,1)}, u32[]{:S(2)}) copy-start(bf16[1,2,384,1024]{3,2,1,0:T(8,128)(2,1)} %param.25) | copy-start | bytes 4718596
  30.4 0.7 %copy-start.3 = (s32[16]{0:T(128)S(1)}, s32[16]{0:T(128)}, u32[]{:S(2)}) copy-start(s32[16]{0:T(128)} %owner.3) | copy-start | bytes 196
  31.1 0.7 %copy-start.5 = (s32[16]{0:T(128)S(1)}, s32[16]{0:T(128)}, u32[]{:S(2)}) copy-start(s32[16]{0:T(128)} %prefix_len.3) | copy-start | bytes 196
  31.8 5.8 %copy-start.1 = (bf16[1024,1024]{1,0:T(8,128)(2,1)S(1)}, bf16[1024,1024]{1,0:T(8,128)(2,1)}, u32[]{:S(2)}) copy-start(bf16[1024,1024]{1,0:T(8,128)(2,1)} %w_out.1) | copy-start | bytes 6291460
  31.8 5.8 %copy-start.4 = (f32[1024]{0:T(1024)S(1)}, f32[1024]{0:T(1024)}, u32[]{:S(2)}) copy-start(f32[1024]{0:T(1024)} %param.28) | copy-start | bytes 12292
  31.8 5.8 %copy-start.6 = (s32[16]{0:T(128)S(1)}, s32[16]{0:T(128)}, u32[]{:S(2)}) copy-start(s32[16]{0:T(128)} %counts.1) | copy-start | bytes 196

commit v4 on v3

--- a/solution.py
+++ b/solution.py
@@ -71,25 +71,24 @@
 
 
 def last_kernel(head, scale, pieces, owner, counts, prefix_len, q, acc, u, gain, w_out, *refs):
-    caches, out, values, total, staged, sems = refs[:pieces], *refs[pieces:]
+    caches, out, total, staged, sems = refs[:pieces], *refs[pieces:]
     slots, width = acc.shape
     length = caches[0].shape[1]
     user = user_here(owner)
     visible = prefix_len[user]
     live = counts[user] - lax.axis_index("helper") * slots
-    for p in range(pieces):
-        values[p] = seen(caches[p][1], piece_base(p + 1, length), visible)
     block = math.gcd(slots, 128)
     copies = []
+    for n in range(width // head):
+        at = slice(n * head, (n + 1) * head)
+        mixed = acc[:, at]
+        for p in range(pieces):
+            weights = weigh(q[:, at], caches[p][0, :, at], scale)
+            part = seen(caches[p][1, :, at], piece_base(p + 1, length), visible)
+            mixed += jnp.dot(weights, part, preferred_element_type=jnp.float32)
+        total[:, at] = mixed
     for first in range(0, slots, block):
         rows = slice(first, first + block)
-        for n in range(width // head):
-            at = slice(n * head, (n + 1) * head)
-            mixed = acc[rows, at]
-            for p in range(pieces):
-                weights = weigh(q[rows, at], caches[p][0, :, at], scale)
-                mixed += jnp.dot(weights, values[p, :, at], preferred_element_type=jnp.float32)
-            total[rows, at] = mixed
         a = total[rows, :]
         centre = a - jnp.mean(a, axis=-1, keepdims=True)
         spread = jnp.mean(centre * centre, axis=-1, keepdims=True)
@@ -149,7 +148,6 @@
         out_specs=pl.BlockSpec(memory_space=pl.ANY),
         out_shape=rows(jnp.bfloat16),
         scratch_shapes=[
-            pltpu.VMEM((pieces, length, width), jnp.bfloat16),
             pltpu.VMEM((slots, width), jnp.float32),
             pltpu.VMEM((slots, width), jnp.bfloat16),
             pltpu.SemaphoreType.DMA((slots // math.gcd(slots, 128),)),

time: 43.2 us -> 41.8 us (0.968)
  waiting for transfers between devices: 21.4 us -> 18.5 us
  starting transfers between devices: 3.76 us -> 6.62 us
  Pallas kernels: 11 us -> 9.63 us
    ppermute x1, waiting for transfers between devices: 21.2 us -> 11.2 us  [turn(): return lambda t: lax.ppermute(t, 'group', pairs)]
    ppermute x1, waiting for transfers between devices: 0.16 us -> 7.29 us  [from_helper(): return lax.ppermute(value, 'helper', pairs)]
    ppermute x1, starting transfers between devices: 0.79 us -> 3.65 us  [turn(): return lambda t: lax.ppermute(t, 'group', pairs)]
    pallas_call x1, Pallas kernels: 5.38 us -> 3.98 us  [local(): pl.pallas_call(functools.partial(last_kernel, head, scale, pieces), in_sp...]
  transfers between devices with their start and end apart: 2 -> 2, of which waited for: 2 -> 2; matrix products, arithmetic and copies ran while one was open for 0% -> 0% of each run, Pallas kernels for 13% -> 14%
where the time goes in v4:
time: 41.8 us; the launch traced here: 41.6 us
  waiting for transfers between devices  18.5 us (44%)
  Pallas kernels  9.63 us (23%)
  starting transfers between devices  6.62 us (16%)
  local copies, waits for them, and re-layouts  6.11 us (15%)
  between operations  0.67 us (2%)
    ppermute x1, waiting for transfers between devices, turn(): return lambda t: lax.ppermute(t, 'group', pairs)  11.2 us
    ppermute x1, waiting for transfers between devices, from_helper(): return lax.ppermute(value, 'helper', pairs)  7.29 us
    unnamed x14, local copies, waits for them, and re-layouts  6.11 us
    pallas_call x1, Pallas kernels, local(): pl.pallas_call(functools.partial(first_kernel, head, scale), in_specs=[sm...  5.65 us
    pallas_call x1, Pallas kernels, local(): pl.pallas_call(functools.partial(last_kernel, head, scale, pieces), in_sp...  3.98 us
    ppermute x1, starting transfers between devices, turn(): return lambda t: lax.ppermute(t, 'group', pairs)  3.65 us
    ppermute x1, starting transfers between devices, from_helper(): return lax.ppermute(value, 'helper', pairs)  2.97 us
  transfers between devices with their start and end apart: 2, of which 2 were waited for; matrix products, arithmetic and copies ran while one was open for 0% of the time, Pallas kernels for 14%

profile of v4, /device:TPU:0, one launch (start us, length us, event | category | flops | bytes accessed | tf_op | source)
XLA Modules:
  0.0 41.6 jit_solution(6651326366706528375)
XLA Ops:
  0.0 3.0 %collective-permute-start.16 = (bf16[2,384,1024]{2,1,0:T(8,128)(2,1)}, bf16[2,384,1024]{2,1,0:T(8,128)(2,1)S(1)}, u32[]{:S(2)}, u32[]{:S(2)}) collective-permute-start(bf16[2,384,1024]{2,1,0:T(8,128)(2,1)} %bitcast.6), channel_id=1, source_target_pairs={{0,1},{1,0},{2,3},{3,2},{4,5},{5,4},{6,7},{7,6},{8,9},{9,8},{10,11... | collective-permute-start | bytes 4718600 | tf_op jit(solution)/shard_map/ppermute | solution.py:118
  3.6 14.9 %conditional.1 = (bf16[256,1024]{1,0:T(8,128)(2,1)}) conditional(s32[]{:T(128)} %bitcast, bf16[256,1024]{1,0:T(8,128)(2,1)} %bitcast.10, bf16[256,1024]{1,0:T(8,128)(2,1)} %bitcast.11, bf16[256,1024]{1,0:T(8,128)(2,1)} %bitcast.12, bf16[256,1024]{1,0:T(8,128)(2,1)} %bitcast.13, ...), branch_computations={%region_0.0_spmd, %region_1.0_spmd, %region_2.0_spmd, %region_3.0_... | conditional | bytes 2097200 | solution.py:126
  3.6 3.7 %collective-permute-start.12 = (bf16[256,1024]{1,0:T(8,128)(2,1)}, bf16[256,1024]{1,0:T(8,128)(2,1)}, u32[]{:S(2)}, u32[]{:S(2)}) collective-permute-start(bf16[256,1024]{1,0:T(8,128)(2,1)} %param.12), channel_id=1, source_target_pairs={{0,24},{2,26},{4,28},{6,30},{8,0},{10,2},{12,4},{14,6},{16,8},{18,... | collective-permute-start | bytes 1572872 | tf_op jit(solution)/shard_map/cond/branch_12_fun/ppermute | solution.py:124
  7.3 11.2 %collective-permute-done.12 = bf16[256,1024]{1,0:T(8,128)(2,1)} collective-permute-done((bf16[256,1024]{1,0:T(8,128)(2,1)}, bf16[256,1024]{1,0:T(8,128)(2,1)}, u32[]{:S(2)}, u32[]{:S(2)}) %collective-permute-start.12) | collective-permute-done | bytes 524320 | tf_op jit(solution)/shard_map/cond/branch_12_fun/ppermute | solution.py:124
  18.5 0.0 copy-start
  18.5 3.4 %copy-done = bf16[1024,4096]{1,0:T(8,128)(2,1)S(1)} copy-done((bf16[1024,4096]{1,0:T(8,128)(2,1)S(1)}, bf16[1024,4096]{1,0:T(8,128)(2,1)}, u32[]{:S(2)}) %copy-start) | copy-done | bytes 8388632
  21.9 0.0 copy-start.2
  21.9 1.4 %copy-done.2 = bf16[1,2,384,1024]{3,2,1,0:T(8,128)(2,1)S(1)} copy-done((bf16[1,2,384,1024]{3,2,1,0:T(8,128)(2,1)S(1)}, bf16[1,2,384,1024]{3,2,1,0:T(8,128)(2,1)}, u32[]{:S(2)}) %copy-start.2) | copy-done | bytes 1572888
  23.3 0.0 copy-start.3
  23.3 0.7 %copy-done.3 = s32[16]{0:T(128)S(1)} copy-done((s32[16]{0:T(128)S(1)}, s32[16]{0:T(128)}, u32[]{:S(2)}) %copy-start.3) | copy-done | bytes 88
  24.0 0.0 copy-start.5
  24.0 0.7 %copy-done.5 = s32[16]{0:T(128)S(1)} copy-done((s32[16]{0:T(128)S(1)}, s32[16]{0:T(128)}, u32[]{:S(2)}) %copy-start.5) | copy-done | bytes 88
  24.6 0.0 copy-start.1
  24.6 0.0 copy-start.4
  24.6 0.0 copy-start.6
  24.6 5.6 %first.1 = (f32[256,1024]{1,0:T(8,128)S(1)}, bf16[256,1024]{1,0:T(8,128)(2,1)S(1)}, f32[256,1024]{1,0:T(8,128)S(1)}) custom-call(s32[16]{0:T(128)S(1)} %copy-done.3, s32[16]{0:T(128)S(1)} %copy-done.5, bf16[256,1024]{1,0:T(8,128)(2,1)} %get-tuple-element.44.tok, bf16[1024,4096]{1,0:T(8,128)(2,1)S(1)} %copy-done, bf16[2,384,1024]{2,1,0:T(8,128)(2,1)S(1)} %bitcast.7), custom_call_target="tpu_custom_call" | custom-call | flops 2550136832 | bytes 13107200 | tf_op jit(solution)/shard_map/first/pallas_call | solution.py:132
  30.3 7.3 %collective-permute-done.16.refs_0_ = bf16[2,384,1024]{2,1,0:T(8,128)(2,1)S(1)} collective-permute-done((bf16[2,384,1024]{2,1,0:T(8,128)(2,1)}, bf16[2,384,1024]{2,1,0:T(8,128)(2,1)S(1)}, u32[]{:S(2)}, u32[]{:S(2)}) %collective-permute-start.16) | collective-permute-done | bytes 1572896 | tf_op jit(solution)/shard_map/ppermute | solution.py:118
  37.6 0.0 copy-done.1
  37.6 0.0 copy-done.4
  37.6 0.0 copy-done.6
  37.6 4.0 %last.1 = bf16[256,1024]{1,0:T(8,128)(2,1)} custom-call(s32[16]{0:T(128)S(1)} %copy-done.3, s32[16]{0:T(128)S(1)} %copy-done.6, s32[16]{0:T(128)S(1)} %copy-done.5, bf16[256,1024]{1,0:T(8,128)(2,1)S(1)} %get-tuple-element.41.q, f32[256,1024]{1,0:T(8,128)S(1)} %get-tuple-element.42.acc, f32[256,1024]{1,0:T(8,128)S(1)} %get-tuple-element.43.u, ...), custom_call_target="tpu_custom_call" | custom-call | flops 939524096 | bytes 3670016 | tf_op jit(solution)/shard_map/last/pallas_call | solution.py:145
Async XLA Ops:
  0.0 37.6 %collective-permute-start.16 = (bf16[2,384,1024]{2,1,0:T(8,128)(2,1)}, bf16[2,384,1024]{2,1,0:T(8,128)(2,1)S(1)}, u32[]{:S(2)}, u32[]{:S(2)}) collective-permute-start(bf16[2,384,1024]{2,1,0:T(8,128)(2,1)} %bitcast.6), channel_id=1, source_target_pairs={{0,1},{1,0},{2,3},{3,2},{4,5},{5,4},{6,7},{7,6},{8,9},{9,8},{10,11... | collective-permute-start | bytes 4718600 | tf_op jit(solution)/shard_map/ppermute | solution.py:118
  3.6 14.9 %collective-permute-start.12 = (bf16[256,1024]{1,0:T(8,128)(2,1)}, bf16[256,1024]{1,0:T(8,128)(2,1)}, u32[]{:S(2)}, u32[]{:S(2)}) collective-permute-start(bf16[256,1024]{1,0:T(8,128)(2,1)} %param.12), channel_id=1, source_target_pairs={{0,24},{2,26},{4,28},{6,30},{8,0},{10,2},{12,4},{14,6},{16,8},{18,... | collective-permute-start | bytes 1572872 | tf_op jit(solution)/shard_map/cond/branch_12_fun/ppermute | solution.py:124
  18.5 3.4 %copy-start = (bf16[1024,4096]{1,0:T(8,128)(2,1)S(1)}, bf16[1024,4096]{1,0:T(8,128)(2,1)}, u32[]{:S(2)}) copy-start(bf16[1024,4096]{1,0:T(8,128)(2,1)} %w.1) | copy-start | bytes 25165828
  21.9 1.4 %copy-start.2 = (bf16[1,2,384,1024]{3,2,1,0:T(8,128)(2,1)S(1)}, bf16[1,2,384,1024]{3,2,1,0:T(8,128)(2,1)}, u32[]{:S(2)}) copy-start(bf16[1,2,384,1024]{3,2,1,0:T(8,128)(2,1)} %param.25) | copy-start | bytes 4718596
  23.3 0.7 %copy-start.3 = (s32[16]{0:T(128)S(1)}, s32[16]{0:T(128)}, u32[]{:S(2)}) copy-start(s32[16]{0:T(128)} %owner.3) | copy-start | bytes 196
  24.0 0.7 %copy-start.5 = (s32[16]{0:T(128)S(1)}, s32[16]{0:T(128)}, u32[]{:S(2)}) copy-start(s32[16]{0:T(128)} %prefix_len.3) | copy-start | bytes 196
  24.6 12.9 %copy-start.1 = (bf16[1024,1024]{1,0:T(8,128)(2,1)S(1)}, bf16[1024,1024]{1,0:T(8,128)(2,1)}, u32[]{:S(2)}) copy-start(bf16[1024,1024]{1,0:T(8,128)(2,1)} %w_out.1) | copy-start | bytes 6291460
  24.6 12.9 %copy-start.4 = (f32[1024]{0:T(1024)S(1)}, f32[1024]{0:T(1024)}, u32[]{:S(2)}) copy-start(f32[1024]{0:T(1024)} %param.28) | copy-start | bytes 12292
  24.6 12.9 %copy-start.6 = (s32[16]{0:T(128)S(1)}, s32[16]{0:T(128)}, u32[]{:S(2)}) copy-start(s32[16]{0:T(128)} %counts.1) | copy-start | bytes 196
